TPU v7x, 32 devices: a whole 2x2x4 slice. The times are simulated.
32 devices in a mesh: row: 4 (over y, x), col: 8 (over z, core).
Axes of the slice: x: 2, y: 2, z: 4, core: 2. Of those that a mesh axis runs over, the one named last changes fastest.
Arguments:
- pair: bfloat16 [128, 128, 128], P('row', 'col'), may hold values from -6 to 6
- cotangent: bfloat16 [128, 128, 128], P('row', 'col'), may hold values from -6 to 6
- token_mask: int32 [128], replicated, may hold values 0 or 1
- out_in_proj: bfloat16 [128, 640], replicated, may hold values from -0.5 to 0.5
- out_out_proj: bfloat16 [128, 128], replicated, may hold values from -0.5 to 0.5
- in_in_proj: bfloat16 [128, 640], replicated, may hold values from -0.5 to 0.5
- in_out_proj: bfloat16 [128, 128], replicated, may hold values from -0.5 to 0.5
Outputs:
- updated_pair: bfloat16 [128, 128, 128], P('row', 'col')
- pair_grad: bfloat16 [128, 128, 128], P('row', 'col')
- out_in_grad: float32 [128, 640], replicated
- out_out_grad: float32 [128, 128], replicated
- in_in_grad: float32 [128, 640], replicated
- in_out_grad: float32 [128, 128], replicated
All inputs are finite; a program needn't handle non-finite values.
Results may differ from a plain program's by a relative error of at most 0.012.
Values may be sent and summed in bfloat16 or wider, within the bound.
No kernel may reach another device: no remote copies, remote signals or barrier semaphores. Data moves between devices by JAX's collectives and lax.ppermute only.
A program may use at most 128 MiB of HBM per device.

v0:
```python
import jax
import jax.numpy as jnp
from jax import lax
from jax.sharding import PartitionSpec as P

H = 128
EPSILON = 1e-05


def shortened(array):
    return jax.tree.map(lambda a: a.astype(jnp.bfloat16) if a.dtype == jnp.float32 else a, array)


def normalize(values):
    centre = jnp.mean(values, axis=-1, keepdims=True)
    shifted = values - centre
    spread = jnp.mean(shifted * shifted, axis=-1, keepdims=True)
    return shifted * lax.rsqrt(spread + EPSILON)


def gating(projected, pair_mask):
    left_value = projected[..., :H]
    left_gate = projected[..., H : 2 * H]
    right_value = projected[..., 2 * H : 3 * H]
    right_gate = projected[..., 3 * H : 4 * H]
    left_full = jax.nn.sigmoid(left_gate) * left_value * pair_mask
    right_full = jax.nn.sigmoid(right_gate) * right_value * pair_mask
    return (left_full, right_full, jax.nn.sigmoid(projected[..., 4 * H :]))


def cols_of(tiles):
    return jax.tree.map(
        lambda part, own: part.astype(own.dtype),
        lax.all_gather(shortened(tiles), "col", axis=1, tiled=True),
        tiles,
    )


def rows_of(tiles):
    return jax.tree.map(
        lambda part, own: part.astype(own.dtype),
        lax.all_gather(shortened(tiles), "row", axis=0, tiled=True),
        tiles,
    )


def to_row_blocks(panel):
    return lax.all_to_all(panel, "col", split_axis=0, concat_axis=1, tiled=True)


def to_col_blocks(panel):
    return lax.all_to_all(panel, "row", split_axis=1, concat_axis=0, tiled=True)


def outgoing_sum(left_tile, right_tile):
    row_panels = rows_of((left_tile, right_tile))
    left_panel = cols_of(left_tile)
    right_rows = to_row_blocks(row_panels[1])
    total = jnp.einsum("ikh,jkh->ijh", left_panel, right_rows, preferred_element_type=jnp.float32)
    return (total, row_panels)


def incoming_sum(left_tile, right_tile):
    col_panels = cols_of((left_tile, right_tile))
    right_all = rows_of(right_tile)
    left_cols = to_col_blocks(col_panels[0])
    total = jnp.einsum("kih,kjh->ijh", left_cols, right_all, preferred_element_type=jnp.float32)
    return (total, col_panels)


def outgoing_grads(tri_grad, row_panels):
    grad_cols = cols_of(tri_grad)
    grad_rows = to_col_blocks(grad_cols)
    left_grad = jnp.einsum(
        "ijh,jkh->ikh", grad_cols, row_panels[1], preferred_element_type=jnp.float32
    )
    right_grad = jnp.einsum(
        "ijh,ikh->jkh", grad_rows, row_panels[0], preferred_element_type=jnp.float32
    )
    return (left_grad, right_grad)


def incoming_grads(tri_grad, col_panels):
    grad_rows = rows_of(tri_grad)
    grad_cols = to_row_blocks(grad_rows)
    left_grad = jnp.einsum(
        "ijh,kjh->kih", grad_cols, col_panels[1], preferred_element_type=jnp.float32
    )
    right_grad = jnp.einsum(
        "kih,ijh->kjh", col_panels[0], grad_rows, preferred_element_type=jnp.float32
    )
    return (left_grad, right_grad)


def forward(pair_in, pair_mask, w_in, w_out, outgoing):
    pair_wide = pair_in.astype(jnp.float32)
    normed = normalize(pair_wide).astype(jnp.bfloat16)
    projected = jnp.dot(normed, w_in, preferred_element_type=jnp.float32)
    left_full, right_full, gate = gating(projected, pair_mask)
    left_tile = left_full.astype(jnp.bfloat16)
    right_tile = right_full.astype(jnp.bfloat16)
    if outgoing:
        triangle_sum, panels = outgoing_sum(left_tile, right_tile)
    else:
        triangle_sum, panels = incoming_sum(left_tile, right_tile)
    tri_normed = normalize(triangle_sum).astype(jnp.bfloat16)
    lifted = jnp.dot(tri_normed, w_out, preferred_element_type=jnp.float32)
    result = (pair_wide + gate * lifted).astype(jnp.bfloat16)
    saved = (pair_wide, normed, projected, gate, triangle_sum, tri_normed, lifted, panels)
    return (result, saved)


def backward(cotan, saved, pair_mask, w_in, w_out, outgoing):
    pair_wide, normed, projected, gate, triangle_sum, tri_normed, lifted, panels = saved
    cot_wide = cotan.astype(jnp.float32)
    lift_grad = gate * cot_wide
    gate_grad = lifted * cot_wide
    out_grad = jnp.einsum(
        "ijh,ijc->hc", tri_normed.astype(jnp.float32), lift_grad, precision=lax.Precision.HIGHEST
    )
    normed_tri_grad = jnp.dot(
        lift_grad, w_out.astype(jnp.float32).T, precision=lax.Precision.HIGHEST
    )
    tri_grad = jax.vjp(normalize, triangle_sum)[1](normed_tri_grad)[0].astype(jnp.bfloat16)
    if outgoing:
        left_grad, right_grad = outgoing_grads(tri_grad, panels)
    else:
        left_grad, right_grad = incoming_grads(tri_grad, panels)
    gate_vjp = jax.vjp(lambda values: gating(values, pair_mask), projected)[1]
    proj_grad = gate_vjp((left_grad, right_grad, gate_grad))[0]
    in_grad = jnp.einsum(
        "ijc,ijq->cq", normed.astype(jnp.float32), proj_grad, precision=lax.Precision.HIGHEST
    )
    normed_grad = jnp.dot(proj_grad, w_in.astype(jnp.float32).T, precision=lax.Precision.HIGHEST)
    pair_grad = (cot_wide + jax.vjp(normalize, pair_wide)[1](normed_grad)[0]).astype(jnp.bfloat16)
    return (pair_grad, in_grad, out_grad)


def local(pair, cotangent, token_mask, out_in_proj, out_out_proj, in_in_proj, in_out_proj):
    row_tile = pair.shape[0]
    col_tile = pair.shape[1]
    row_flags = lax.dynamic_slice_in_dim(
        token_mask, lax.axis_index("row") * row_tile, row_tile, 0
    ).astype(jnp.float32)
    col_flags = lax.dynamic_slice_in_dim(
        token_mask, lax.axis_index("col") * col_tile, col_tile, 0
    ).astype(jnp.float32)
    pair_mask = (row_flags[:, None] * col_flags[None, :])[:, :, None]
    middle, saved_out = forward(pair, pair_mask, out_in_proj, out_out_proj, True)
    updated, saved_in = forward(middle, pair_mask, in_in_proj, in_out_proj, False)
    middle_grad, in_in_part, in_out_part = backward(
        cotangent, saved_in, pair_mask, in_in_proj, in_out_proj, False
    )
    pair_grad, out_in_part, out_out_part = backward(
        middle_grad, saved_out, pair_mask, out_in_proj, out_out_proj, True
    )
    totals = lax.psum((out_in_part, out_out_part, in_in_part, in_out_part), ("row", "col"))
    tokens_all = row_tile * lax.axis_size("row")
    return (
        updated,
        pair_grad,
        totals[0] / tokens_all,
        totals[1] / tokens_all,
        totals[2] / tokens_all,
        totals[3] / tokens_all,
    )


def solution(mesh):
    return jax.shard_map(
        local,
        mesh=mesh,
        in_specs=(P("row", "col", None), P("row", "col", None), P(), P(), P(), P(), P()),
        out_specs=(P("row", "col", None), P("row", "col", None), P(), P(), P(), P()),
        check_vma=False,
    )
```

profile of v0, /device:TPU:0, one launch (start us, length us, event | category | flops | bytes accessed | tf_op | source)
XLA Modules:
  0.0 431.3 jit_solution(16462402712832531715)
XLA Ops:
  14.1 11.5 %all_gather.24 = bf16[128,16,128]{2,1,0:T(8,128)(2,1)S(1)} all-gather(bf16[32,16,128]{2,1,0:T(8,128)(2,1)S(1)} %get-tuple-element.33), channel_id=1, replica_groups=mesh['row'=4,'col'=8] {'row'}, dimensions={0}, use_global_device_ids=true | all-gather | bytes 655360 | tf_op jit(solution)/shard_map/all_gather | solution.py:42
  25.6 23.7 %all_to_all.72 = bf16[128,16,128]{2,1,0:T(8,128)(2,1)S(1)} all-to-all(bf16[128,16,128]{2,1,0:T(8,128)(2,1)S(1)} %all_gather.24), channel_id=1, replica_groups=mesh['row'=4,'col'=8] {'col'}, dimensions={0} | all-to-all | bytes 1048576 | tf_op jit(solution)/shard_map/all_to_all | solution.py:48
  50.6 8.6 %copy.223 = bf16[32,128,128]{0,1,2:T(8,128)(2,1)} copy(bf16[32,128,128]{2,1,0:T(8,128)(2,1)} %all-gather.5.cloned.1.call-done) | data formatting | bytes 2097152 | tf_op jit(solution)/shard_map/all_gather | solution.py:34
  59.2 3.6 bitcast_reduce_fusion.1
  69.5 22.5 %all-gather.7.cloned.1.call-done = bf16[32,128,128]{2,1,0:T(8,128)(2,1)} async-done(((bf16[32,16,128]{2,1,0:T(8,128)(2,1)}), bf16[32,128,128]{2,1,0:T(8,128)(2,1)}) %all-gather.7.cloned.1.call-update) | async-done | bytes 1048592 | tf_op jit(solution)/shard_map/all_gather | solution.py:34
  92.1 2.9 copy.233
  94.9 4.2 all-to-all-start.1
  99.9 19.8 %all_gather.26 = bf16[128,16,128]{2,1,0:T(8,128)(2,1)} all-gather(bf16[32,16,128]{2,1,0:T(8,128)(2,1)} %get-tuple-element.31), channel_id=1, replica_groups=mesh['row'=4,'col'=8] {'row'}, dimensions={0}, use_global_device_ids=true | all-gather | bytes 655360 | tf_op jit(solution)/shard_map/all_gather | solution.py:42
  124.9 3.2 copy.237
  128.1 3.0 bitcast_reduce_fusion
  134.8 2.7 multiply_reduce_fusion.1
  151.8 9.8 %all_gather.28 = bf16[128,16,128]{2,1,0:T(8,128)(2,1)} all-gather(bf16[32,16,128]{2,1,0:T(8,128)(2,1)S(1)} %add_convert_fusion.1), channel_id=1, replica_groups=mesh['row'=4,'col'=8] {'row'}, dimensions={0}, use_global_device_ids=true | all-gather | bytes 655360 | tf_op jit(solution)/shard_map/all_gather | solution.py:42
  161.6 4.1 all-to-all-start.2
  166.0 8.6 %copy.248 = bf16[32,128,128]{0,1,2:T(8,128)(2,1)} copy(bf16[32,128,128]{2,1,0:T(8,128)(2,1)} %all-gather.7.cloned.1.call-done) | data formatting | bytes 2097152 | tf_op jit(solution)/shard_map/all_gather | solution.py:34
  174.6 8.6 %copy.251 = bf16[32,128,128]{0,1,2:T(8,128)(2,1)} copy(bf16[32,128,128]{2,1,0:T(8,128)(2,1)} %all-gather.9.cloned.1.call-done) | data formatting | bytes 2097152 | tf_op jit(solution)/shard_map/all_gather | solution.py:34
  185.7 4.6 %fusion.83 = f32[128,16,32]{2,1,0:T(8,128)} fusion(bf16[128,16,128]{0,1,2:T(8,128)(2,1)} %copy.247, bf16[32,128,128]{0,1,2:T(8,128)(2,1)} %copy.248), kind=kOutput, calls=%fused_computation.151 | convolution fusion | flops 16777216 | bytes 1835008 | tf_op jit(solution)/shard_map/kih,ijh->kjh/dot_general | solution.py:89
  196.8 4.5 %fusion.86 = f32[128,32,16]{1,2,0:T(8,128)} fusion(bf16[16,128,128]{1,0,2:T(8,128)(2,1)} %copy.252, bf16[32,128,128]{0,1,2:T(8,128)(2,1)} %copy.251), kind=kOutput, calls=%fused_computation.154 | convolution fusion | flops 16777216 | bytes 1835008 | tf_op jit(solution)/shard_map/ijh,kjh->kih/dot_general | solution.py:86
  234.0 10.2 %all_gather.30 = bf16[128,16,128]{2,1,0:T(8,128)(2,1)S(1)} all-gather(bf16[32,16,128]{2,1,0:T(8,128)(2,1)} %get-tuple-element.32), channel_id=1, replica_groups=mesh['row'=4,'col'=8] {'row'}, dimensions={0}, use_global_device_ids=true | all-gather | bytes 655360 | tf_op jit(solution)/shard_map/all_gather | solution.py:42
  245.6 11.2 %all-gather.11.cloned.1.call-done = bf16[32,128,128]{2,1,0:T(8,128)(2,1)} async-done(((bf16[32,16,128]{2,1,0:T(8,128)(2,1)}), bf16[32,128,128]{2,1,0:T(8,128)(2,1)}) %all-gather.11.cloned.1.call-update) | async-done | bytes 1048592 | tf_op jit(solution)/shard_map/all_gather | solution.py:34
  256.8 2.9 copy.262
  259.7 4.4 %all-to-all-start.3 = ((bf16[32,128,128]{2,0,1:T(8,128)(2,1)}), bf16[32,128,128]{2,0,1:T(8,128)(2,1)}, u32[]{:S(2)}, u32[]{:S(2)}) async-start(bf16[32,128,128]{2,0,1:T(8,128)(2,1)} %copy.262), calls=%async_computation.3 | async-start | bytes 2097152 | tf_op jit(solution)/shard_map/all_to_all | solution.py:52
  269.3 6.8 %copy.269 = bf16[32,128,128]{0,1,2:T(8,128)(2,1)} copy(bf16[32,128,128]{2,1,0:T(8,128)(2,1)S(1)} %copy-done.1) | data formatting | bytes 2097152 | tf_op jit(solution)/shard_map/all_gather | solution.py:34
  276.1 3.4 fusion.85
  291.5 129.8 %all-reduce.13.cloned.1.call-done = (f32[128,640]{1,0:T(8,128)}, f32[128,128]{1,0:T(8,128)}, f32[128,640]{1,0:T(8,128)}, f32[128,128]{1,0:T(8,128)}) async-done(((f32[128,640]{1,0:T(8,128)}, f32[128,128]{1,0:T(8,128)}, f32[128,640]{1,0:T(8,128)}, f32[128,128]{1,0:T(8,128)}), (f32[128,640]{1,0:T(8,128)}, f32[128,128]{1,0:T(8,128)}, f32[128,640]{1,0:T(8,128)}, ...) | async-done | bytes 786448 | tf_op jit(solution)/shard_map/psum | solution.py:157
  (181 shorter events, 102.4 us)
Async XLA Ops:
  7.2 60.2 %copy-start = (bf16[128,640]{1,0:T(8,128)(2,1)S(1)}, bf16[128,640]{1,0:T(8,128)(2,1)}, u32[]{:S(2)}) copy-start(bf16[128,640]{1,0:T(8,128)(2,1)} %param.12) | copy-start | bytes 491524
  7.2 43.4 %all-gather.5.cloned.1.call-start = ((), (), s32[]{:S(2)}) async-start(), calls=%async_computation.4 | async-start | bytes 1179648 | tf_op jit(solution)/shard_map/all_gather | solution.py:34
  14.1 78.0 %all-gather.7.cloned.1.call-start = ((), (), s32[]{:S(2)}) async-start(), calls=%async_computation.5 | async-start | bytes 1179648 | tf_op jit(solution)/shard_map/all_gather | solution.py:34
  63.3 4.0 copy-start.2
  94.9 27.3 %all-to-all-start.1 = ((bf16[32,128,128]{2,0,1:T(8,128)(2,1)}), bf16[32,128,128]{2,0,1:T(8,128)(2,1)}, u32[]{:S(2)}, u32[]{:S(2)}) async-start(bf16[32,128,128]{2,0,1:T(8,128)(2,1)} %copy.233), calls=%async_computation.1 | async-start | bytes 2097152 | tf_op jit(solution)/shard_map/all_to_all | solution.py:52
  99.2 75.4 %all-gather.9.cloned.1.call-start = ((), (), s32[]{:S(2)}) async-start(), calls=%async_computation.6 | async-start | bytes 1179648 | tf_op jit(solution)/shard_map/all_gather | solution.py:34
  134.8 68.9 %copy-start.19 = (f32[32,16]{1,0:T(8,128)}, f32[32,16]{1,0:T(8,128)S(1)}, u32[]{:S(2)}) copy-start(f32[32,16]{1,0:T(8,128)S(1)} %copy.240) | copy-start | bytes 6148
  161.6 31.0 %all-to-all-start.2 = ((bf16[128,16,128]{2,1,0:T(8,128)(2,1)}), bf16[128,16,128]{2,1,0:T(8,128)(2,1)}, u32[]{:S(2)}, u32[]{:S(2)}) async-start(bf16[128,16,128]{2,1,0:T(8,128)(2,1)} %all_gather.28), calls=%async_computation.2 | async-start | bytes 1048576 | tf_op jit(solution)/shard_map/all_to_all | solution.py:48
  165.8 91.0 %all-gather.11.cloned.1.call-start = ((), (), s32[]{:S(2)}) async-start(), calls=%async_computation.7 | async-start | bytes 1179648 | tf_op jit(solution)/shard_map/all_gather | solution.py:34
  203.7 2.4 copy-start.8
  206.1 2.1 copy-start.26
  206.1 2.1 copy-start.28
  206.1 2.1 copy-start.30
  206.1 2.9 copy-start.24
  216.4 2.2 copy-start.3
  216.4 2.2 copy-start.25
  218.6 5.7 %copy-start.18 = (f32[32,16]{1,0:T(8,128)S(1)}, f32[32,16]{1,0:T(8,128)}, u32[]{:S(2)}) copy-start(f32[32,16]{1,0:T(8,128)} %copy-done.17) | copy-start | bytes 6148
  259.7 4.7 %copy-start.6 = (f32[128,16,32]{0,1,2:T(8,128)S(1)}, f32[128,16,32]{0,1,2:T(8,128)}, u32[]{:S(2)}) copy-start(f32[128,16,32]{0,1,2:T(8,128)} %copy.238) | copy-start | bytes 786436
  259.7 20.3 %all-to-all-start.3 = ((bf16[32,128,128]{2,0,1:T(8,128)(2,1)}), bf16[32,128,128]{2,0,1:T(8,128)(2,1)}, u32[]{:S(2)}, u32[]{:S(2)}) async-start(bf16[32,128,128]{2,0,1:T(8,128)(2,1)} %copy.262), calls=%async_computation.3 | async-start | bytes 2097152 | tf_op jit(solution)/shard_map/all_to_all | solution.py:52
  264.1 2.4 copy-start.4
  264.1 157.2 %all-reduce.13.cloned.1.call-start = ((), (), s32[]{:S(2)}) async-start(), calls=%async_computation.8 | async-start | bytes 1572864 | tf_op jit(solution)/shard_map/psum | solution.py:157
  264.4 2.1 copy-start.13
  269.3 6.8 %copy-start.11 = (bf16[128,16,128]{0,1,2:T(8,128)(2,1)S(1)}, bf16[128,16,128]{0,1,2:T(8,128)(2,1)}, u32[]{:S(2)}) copy-start(bf16[128,16,128]{0,1,2:T(8,128)(2,1)} %copy.268) | copy-start | bytes 1572868
  281.6 2.3 copy-start.10
  (20 other events, 25.1 us)
Sparse Core Ops, SparseCore 0:
  14.2 32.2 all-gather.4
  69.6 22.3 all-gather.6
  101.6 24.2 all-gather.8
  232.6 24.2 all-gather.10
  290.4 130.9 all-reduce.12
where the time goes:
time: 434 us; the launch traced here: 431 us
  waiting for transfers between devices  164 us (38%)
  local copies, waits for them, and re-layouts  92.8 us (21%)
  blocking collectives  75.1 us (17%)
  matrix products  41.1 us (9%)
  other arithmetic  30.4 us (7%)
  between operations  14.2 us (3%)
  starting transfers between devices  13.4 us (3%)
    psum x1, waiting for transfers between devices, local(): lax.psum((out_in_part, out_out_part, in_in_part, in_out_part), ('row', 'c...  130 us
    all_gather x4, blocking collectives, rows_of(): lax.all_gather(shortened(tiles), 'row', axis=0, tiled=True)  51.3 us
    all_gather x6, local copies, waits for them, and re-layouts, cols_of(): lax.all_gather(shortened(tiles), 'col', axis=1, tiled=True)  38.3 us
    all_gather x4, waiting for transfers between devices, cols_of(): lax.all_gather(shortened(tiles), 'col', axis=1, tiled=True)  33.8 us
    all_to_all x1, blocking collectives, to_row_blocks(): return lax.all_to_all(panel, 'col', split_axis=0, concat_axis=1, tiled=True)  23.7 us
    unnamed x78, local copies, waits for them, and re-layouts  9.87 us
    all_to_all x4, local copies, waits for them, and re-layouts, to_col_blocks(): return lax.all_to_all(panel, 'row', split_axis=1, concat_axis=0, tiled=True)  9.75 us
  transfers between devices with their start and end apart: 8, of which 3 were waited for; matrix products, arithmetic and copies ran while one was open for 18% of the time, Pallas kernels for 0%

commit v1 on v0

--- a/solution.py
+++ b/solution.py
@@ -45,7 +45,10 @@
 
 
 def to_row_blocks(panel):
-    return lax.all_to_all(panel, "col", split_axis=0, concat_axis=1, tiled=True)
+    return jnp.concatenate(
+        lax.all_to_all(jnp.stack(jnp.split(panel, lax.axis_size("col"), axis=0)), "col", 0, 0),
+        axis=1,
+    )
 
 
 def to_col_blocks(panel):

time: 434 us -> 403 us (0.929)
  local copies, waits for them, and re-layouts: 92.8 us -> 78.4 us
  other arithmetic: 30.4 us -> 18.4 us
    unnamed x78 -> x100, local copies, waits for them, and re-layouts: 9.87 us -> 9.82 us
where the time goes in v1:
time: 403 us; the launch traced here: 401 us
  waiting for transfers between devices  164 us (41%)
  local copies, waits for them, and re-layouts  78.4 us (19%)
  blocking collectives  74.7 us (19%)
  matrix products  37.7 us (9%)
  other arithmetic  18.4 us (5%)
  between operations  14.3 us (4%)
  starting transfers between devices  13.4 us (3%)
    psum x1, waiting for transfers between devices, local(): lax.psum((out_in_part, out_out_part, in_in_part, in_out_part), ('row', 'c...  130 us
    all_gather x4, blocking collectives, rows_of(): lax.all_gather(shortened(tiles), 'row', axis=0, tiled=True)  51.2 us
    all_gather x6, local copies, waits for them, and re-layouts, cols_of(): lax.all_gather(shortened(tiles), 'col', axis=1, tiled=True)  38.3 us
    all_gather x4, waiting for transfers between devices, cols_of(): lax.all_gather(shortened(tiles), 'col', axis=1, tiled=True)  33.8 us
    all_to_all x1, blocking collectives, to_row_blocks(): lax.all_to_all(jnp.stack(jnp.split(panel, lax.axis_size('col'), axis=0)),...  23.6 us
    unnamed x100, local copies, waits for them, and re-layouts  9.82 us
    all_to_all x4, local copies, waits for them, and re-layouts, to_col_blocks(): return lax.all_to_all(panel, 'row', split_axis=1, concat_axis=0, tiled=True)  9.75 us
    all_to_all x2, starting transfers between devices, to_col_blocks(): return lax.all_to_all(panel, 'row', split_axis=1, concat_axis=0, tiled=True)  8.62 us
  transfers between devices with their start and end apart: 8, of which 3 were waited for; matrix products, arithmetic and copies ran while one was open for 18% of the time, Pallas kernels for 0%

profile of v1, /device:TPU:0, one launch (start us, length us, event | category | flops | bytes accessed | tf_op | source)
XLA Modules:
  0.0 401.3 jit_solution(14780847981704059782)
XLA Ops:
  14.1 11.5 %all_gather.24 = bf16[128,16,128]{2,1,0:T(8,128)(2,1)S(1)} all-gather(bf16[32,16,128]{2,1,0:T(8,128)(2,1)S(1)} %get-tuple-element.33), channel_id=1, replica_groups=mesh['row'=4,'col'=8] {'row'}, dimensions={0}, use_global_device_ids=true | all-gather | bytes 655360 | tf_op jit(solution)/shard_map/all_gather | solution.py:42
  25.8 23.6 %all_to_all.46 = bf16[8,16,16,128]{3,2,1,0:T(8,128)(2,1)S(1)} all-to-all(bf16[8,16,16,128]{3,2,1,0:T(8,128)(2,1)S(1)} %fusion.69), channel_id=1, replica_groups=mesh['row'=4,'col'=8] {'col'}, dimensions={0} | all-to-all | bytes 1048576 | tf_op jit(solution)/shard_map/all_to_all | solution.py:49
  50.6 8.6 %copy.215 = bf16[32,128,128]{0,1,2:T(8,128)(2,1)} copy(bf16[32,128,128]{2,1,0:T(8,128)(2,1)} %all-gather.5.cloned.1.call-done) | data formatting | bytes 2097152 | tf_op jit(solution)/shard_map/all_gather | solution.py:34
  59.2 3.6 bitcast_reduce_fusion.1
  69.8 22.6 %all-gather.7.cloned.1.call-done = bf16[32,128,128]{2,1,0:T(8,128)(2,1)} async-done(((bf16[32,16,128]{2,1,0:T(8,128)(2,1)}), bf16[32,128,128]{2,1,0:T(8,128)(2,1)}) %all-gather.7.cloned.1.call-update) | async-done | bytes 1048592 | tf_op jit(solution)/shard_map/all_gather | solution.py:34
  92.4 2.9 copy.225
  95.3 4.2 %all-to-all-start.1 = ((bf16[32,128,128]{2,0,1:T(8,128)(2,1)}), bf16[32,128,128]{2,0,1:T(8,128)(2,1)}, u32[]{:S(2)}, u32[]{:S(2)}) async-start(bf16[32,128,128]{2,0,1:T(8,128)(2,1)} %copy.225), calls=%async_computation.1 | async-start | bytes 2097152 | tf_op jit(solution)/shard_map/all_to_all | solution.py:55
  100.3 19.8 %all_gather.26 = bf16[128,16,128]{2,1,0:T(8,128)(2,1)} all-gather(bf16[32,16,128]{2,1,0:T(8,128)(2,1)} %get-tuple-element.31), channel_id=1, replica_groups=mesh['row'=4,'col'=8] {'row'}, dimensions={0}, use_global_device_ids=true | all-gather | bytes 655360 | tf_op jit(solution)/shard_map/all_gather | solution.py:42
  125.2 3.2 copy.229
  128.4 3.1 bitcast_reduce_fusion
  135.2 2.7 multiply_reduce_fusion.1
  142.6 9.1 %all_gather.28 = bf16[128,16,128]{2,1,0:T(8,128)(2,1)S(1)} all-gather(bf16[32,16,128]{2,1,0:T(8,128)(2,1)S(1)} %add_convert_fusion.1), channel_id=1, replica_groups=mesh['row'=4,'col'=8] {'row'}, dimensions={0}, use_global_device_ids=true | all-gather | bytes 655360 | tf_op jit(solution)/shard_map/all_gather | solution.py:42
  156.6 4.1 %all-to-all-start.2 = ((bf16[8,16,16,128]{3,2,1,0:T(8,128)(2,1)}), bf16[8,16,16,128]{3,2,1,0:T(8,128)(2,1)}, u32[]{:S(2)}, u32[]{:S(2)}) async-start(bf16[8,16,16,128]{3,2,1,0:T(8,128)(2,1)} %fusion.61), calls=%async_computation.2 | async-start | bytes 1048576 | tf_op jit(solution)/shard_map/all_to_all | solution.py:49
  161.0 8.6 %copy.240 = bf16[32,128,128]{0,1,2:T(8,128)(2,1)} copy(bf16[32,128,128]{2,1,0:T(8,128)(2,1)} %all-gather.7.cloned.1.call-done) | data formatting | bytes 2097152 | tf_op jit(solution)/shard_map/all_gather | solution.py:34
  169.6 8.6 %copy.243 = bf16[32,128,128]{0,1,2:T(8,128)(2,1)} copy(bf16[32,128,128]{2,1,0:T(8,128)(2,1)} %all-gather.9.cloned.1.call-done) | data formatting | bytes 2097152 | tf_op jit(solution)/shard_map/all_gather | solution.py:34
  179.7 3.5 fusion.99
  186.8 3.5 fusion.102
  203.5 10.7 %all_gather.30 = bf16[128,16,128]{2,1,0:T(8,128)(2,1)S(1)} all-gather(bf16[32,16,128]{2,1,0:T(8,128)(2,1)S(1)} %copy-done.11), channel_id=1, replica_groups=mesh['row'=4,'col'=8] {'row'}, dimensions={0}, use_global_device_ids=true | all-gather | bytes 655360 | tf_op jit(solution)/shard_map/all_gather | solution.py:42
  215.7 11.2 %all-gather.11.cloned.1.call-done = bf16[32,128,128]{2,1,0:T(8,128)(2,1)} async-done(((bf16[32,16,128]{2,1,0:T(8,128)(2,1)}), bf16[32,128,128]{2,1,0:T(8,128)(2,1)}) %all-gather.11.cloned.1.call-update) | async-done | bytes 1048592 | tf_op jit(solution)/shard_map/all_gather | solution.py:34
  226.8 2.9 copy.254
  229.7 4.4 %all-to-all-start.3 = ((bf16[32,128,128]{2,0,1:T(8,128)(2,1)}), bf16[32,128,128]{2,0,1:T(8,128)(2,1)}, u32[]{:S(2)}, u32[]{:S(2)}) async-start(bf16[32,128,128]{2,0,1:T(8,128)(2,1)} %copy.254), calls=%async_computation.3 | async-start | bytes 2097152 | tf_op jit(solution)/shard_map/all_to_all | solution.py:55
  239.2 6.8 %copy.261 = bf16[32,128,128]{0,1,2:T(8,128)(2,1)} copy(bf16[32,128,128]{2,1,0:T(8,128)(2,1)S(1)} %copy-done.2) | data formatting | bytes 2097152 | tf_op jit(solution)/shard_map/all_gather | solution.py:34
  246.0 3.4 fusion.101
  261.4 129.9 %all-reduce.13.cloned.1.call-done = (f32[128,640]{1,0:T(8,128)}, f32[128,128]{1,0:T(8,128)}, f32[128,640]{1,0:T(8,128)}, f32[128,128]{1,0:T(8,128)}) async-done(((f32[128,640]{1,0:T(8,128)}, f32[128,128]{1,0:T(8,128)}, f32[128,640]{1,0:T(8,128)}, f32[128,128]{1,0:T(8,128)}), (f32[128,640]{1,0:T(8,128)}, f32[128,128]{1,0:T(8,128)}, f32[128,640]{1,0:T(8,128)}, ...) | async-done | bytes 786448 | tf_op jit(solution)/shard_map/psum | solution.py:160
  (205 shorter events, 74.6 us)
Async XLA Ops:
  7.2 60.2 %copy-start = (bf16[128,640]{1,0:T(8,128)(2,1)S(1)}, bf16[128,640]{1,0:T(8,128)(2,1)}, u32[]{:S(2)}) copy-start(bf16[128,640]{1,0:T(8,128)(2,1)} %param.12) | copy-start | bytes 491524
  7.2 43.4 %all-gather.5.cloned.1.call-start = ((), (), s32[]{:S(2)}) async-start(), calls=%async_computation.4 | async-start | bytes 1179648 | tf_op jit(solution)/shard_map/all_gather | solution.py:34
  14.1 78.3 %all-gather.7.cloned.1.call-start = ((), (), s32[]{:S(2)}) async-start(), calls=%async_computation.5 | async-start | bytes 1179648 | tf_op jit(solution)/shard_map/all_gather | solution.py:34
  63.3 4.0 copy-start.3
  64.4 1.9 copy-start.17
  68.6 66.6 %copy-start.1 = (f32[32,16,640]{2,1,0:T(8,128)}, f32[32,16,640]{2,1,0:T(8,128)S(1)}, u32[]{:S(2)}) copy-start(f32[32,16,640]{2,1,0:T(8,128)S(1)} %fusion.50) | copy-start | bytes 3932164
  95.3 27.3 %all-to-all-start.1 = ((bf16[32,128,128]{2,0,1:T(8,128)(2,1)}), bf16[32,128,128]{2,0,1:T(8,128)(2,1)}, u32[]{:S(2)}, u32[]{:S(2)}) async-start(bf16[32,128,128]{2,0,1:T(8,128)(2,1)} %copy.225), calls=%async_computation.1 | async-start | bytes 2097152 | tf_op jit(solution)/shard_map/all_to_all | solution.py:55
  99.5 70.1 %all-gather.9.cloned.1.call-start = ((), (), s32[]{:S(2)}) async-start(), calls=%async_computation.6 | async-start | bytes 1179648 | tf_op jit(solution)/shard_map/all_gather | solution.py:34
  135.2 56.3 %copy-start.19 = (f32[32,16]{1,0:T(8,128)}, f32[32,16]{1,0:T(8,128)S(1)}, u32[]{:S(2)}) copy-start(f32[32,16]{1,0:T(8,128)S(1)} %copy.232) | copy-start | bytes 6148
  139.6 1.6 copy-start.21
  156.6 27.8 %all-to-all-start.2 = ((bf16[8,16,16,128]{3,2,1,0:T(8,128)(2,1)}), bf16[8,16,16,128]{3,2,1,0:T(8,128)(2,1)}, u32[]{:S(2)}, u32[]{:S(2)}) async-start(bf16[8,16,16,128]{3,2,1,0:T(8,128)(2,1)} %fusion.61), calls=%async_computation.2 | async-start | bytes 1048576 | tf_op jit(solution)/shard_map/all_to_all | solution.py:49
  160.8 66.1 %all-gather.11.cloned.1.call-start = ((), (), s32[]{:S(2)}) async-start(), calls=%async_computation.7 | async-start | bytes 1179648 | tf_op jit(solution)/shard_map/all_gather | solution.py:34
  191.5 3.4 copy-start.8
  194.9 2.2 copy-start.14
  195.7 3.3 copy-start.4
  199.0 37.5 %copy-start.12 = (bf16[32,16,128]{2,1,0:T(8,128)(2,1)}, bf16[32,16,128]{2,1,0:T(8,128)(2,1)S(1)}, u32[]{:S(2)}) copy-start(bf16[32,16,128]{2,1,0:T(8,128)(2,1)S(1)} %get-tuple-element.13) | copy-start | bytes 393220
  200.3 3.2 copy-start.11
  229.7 4.7 %copy-start.20 = (f32[32,16]{1,0:T(8,128)S(1)}, f32[32,16]{1,0:T(8,128)}, u32[]{:S(2)}) copy-start(f32[32,16]{1,0:T(8,128)} %copy-done.19) | copy-start | bytes 6148
  229.7 4.7 %copy-start.22 = (f32[32,16]{1,0:T(8,128)S(1)}, f32[32,16]{1,0:T(8,128)}, u32[]{:S(2)}) copy-start(f32[32,16]{1,0:T(8,128)} %copy-done.21) | copy-start | bytes 6148
  229.7 4.7 %copy-start.23 = (bf16[32,16,128]{2,1,0:T(8,128)(2,1)S(1)}, bf16[32,16,128]{2,1,0:T(8,128)(2,1)}, u32[]{:S(2)}) copy-start(bf16[32,16,128]{2,1,0:T(8,128)(2,1)} %param.8) | copy-start | bytes 393220
  229.7 20.2 %all-to-all-start.3 = ((bf16[32,128,128]{2,0,1:T(8,128)(2,1)}), bf16[32,128,128]{2,0,1:T(8,128)(2,1)}, u32[]{:S(2)}, u32[]{:S(2)}) async-start(bf16[32,128,128]{2,0,1:T(8,128)(2,1)} %copy.254), calls=%async_computation.3 | async-start | bytes 2097152 | tf_op jit(solution)/shard_map/all_to_all | solution.py:55
  234.1 157.2 %all-reduce.13.cloned.1.call-start = ((), (), s32[]{:S(2)}) async-start(), calls=%async_computation.8 | async-start | bytes 1572864 | tf_op jit(solution)/shard_map/psum | solution.py:160
  239.2 6.8 %copy-start.10 = (bf16[128,16,128]{0,1,2:T(8,128)(2,1)S(1)}, bf16[128,16,128]{0,1,2:T(8,128)(2,1)}, u32[]{:S(2)}) copy-start(bf16[128,16,128]{0,1,2:T(8,128)(2,1)} %copy.260) | copy-start | bytes 1572868
  251.5 2.3 copy-start.9
  (24 other events, 27.8 us)
Sparse Core Ops, SparseCore 0:
  14.2 32.2 all-gather.4
  69.9 22.4 all-gather.6
  101.9 24.2 all-gather.8
  202.1 24.7 all-gather.10
  260.2 130.9 all-reduce.12
